TPU v7x, 32 devices: a whole 2x2x4 slice. The times are simulated.
32 devices in a mesh: dp: 4 (over y, x), expert: 8 (over z, core).
Axes of the slice: x: 2, y: 2, z: 4, core: 2. Of those that a mesh axis runs over, the one named last changes fastest.
Arguments:
- residual: bfloat16 [2048, 1024], P(('dp', 'expert')), parts along dimension 0, may hold values from -6 to 6
- expert_ids: int32 [2048, 8], P(('dp', 'expert')), parts along dimension 0, may hold values from 0 to 63, all different within a row; in each aligned block of 64 rows (0 to 63, 64 to 127, ...) at most 12 rows name the same one
- route_weights: float32 [2048, 8], P(('dp', 'expert')), parts along dimension 0, may hold values from 0.05 to 0.5
- expert_out: bfloat16 [24576, 1024], P(('dp', 'expert')), parts along dimension 0, may hold values from -6 to 6
Outputs:
- mixed: bfloat16 [2048, 1024], P(('dp', 'expert')), parts along dimension 0
- expert_load: float32 [256], P('dp'), parts along dimension 0
There are 4 independent parts, one for each index of `dp`. A program takes and returns all parts, laid end to end along the dimension named above; each array names one. Nothing has to cross between parts.
Inputs may be any that keep to these rules, and one draw needn't show every extreme that they name: `expert_ids`: each row names 8 different experts. Within the rows of one device no expert is named by more than 12 rows, and in some devices' rows an expert is named by exactly 12.
All inputs are finite; a program needn't handle non-finite values.
Results may differ from a plain program's by a relative error of at most 0.001.
Values may be sent and summed in bfloat16 or wider, within the bound.
A program may use at most 64 MiB of HBM per device.

v0:
```python
import jax
import jax.numpy as jnp
from jax import lax
from jax.sharding import PartitionSpec as P

EXPERTS = 64


def per_device(residual, expert_ids, route_weights, expert_out):
    peers = lax.axis_size("expert")
    per_peer = expert_out.shape[0] // peers
    width = residual.shape[1]
    tokens_here = expert_ids.shape[0]
    fanout = expert_ids.shape[1]
    capacity = expert_out.shape[0] // EXPERTS
    routes = expert_ids.reshape(-1)
    onehot = (routes[:, None] == jnp.arange(EXPERTS, dtype=jnp.int32)[None, :]).astype(jnp.int32)
    earlier = jnp.cumsum(onehot, axis=0, dtype=jnp.int32) - onehot
    slots = jnp.sum(earlier * onehot, axis=1, dtype=jnp.int32)
    source_rows = routes * capacity + slots
    own_counts = jnp.sum(onehot, axis=0).astype(jnp.float32)
    column_blocks = 2
    block_width = width // column_blocks
    blocks = expert_out.reshape(peers, per_peer, column_blocks, block_width)
    load_totals = lax.psum(own_counts, "expert")
    arrived = lax.all_to_all(blocks, "expert", split_axis=0, concat_axis=0, tiled=True)
    several = arrived.shape[2]
    stacked = arrived.reshape(peers * per_peer, several, arrived.shape[3])
    picked = jnp.take(stacked, source_rows, axis=0).reshape(
        tokens_here, fanout, several, arrived.shape[3]
    )
    total = jnp.zeros((tokens_here, several, arrived.shape[3]), jnp.float32)
    for choice_index in range(fanout):
        total = total + route_weights[:, choice_index, None, None] * picked[:, choice_index].astype(
            jnp.float32
        )
    mixed = (total.reshape(tokens_here, width) + residual.astype(jnp.float32)).astype(jnp.bfloat16)
    return (mixed, load_totals)


def solution(mesh):
    placed = (
        P(("dp", "expert"), None),
        P(("dp", "expert"), None),
        P(("dp", "expert"), None),
        P(("dp", "expert"), None),
    )
    return jax.shard_map(
        per_device,
        mesh=mesh,
        in_specs=placed,
        out_specs=(P(("dp", "expert"), None), P("dp")),
        check_vma=False,
    )
```

profile of v0, /device:TPU:16, one launch (start us, length us, event | category | flops | bytes accessed | tf_op | source)
XLA Modules:
  0.0 60.8 jit_solution(4603753391468910772)
XLA Ops:
  0.6 3.9 %reshape.104 = bf16[8,96,2,512]{3,2,1,0:T(2,128)(2,1)} reshape(bf16[768,1024]{1,0:T(8,128)(2,1)} %param.7) | data formatting | bytes 3145728 | tf_op jit(solution)/shard_map/reshape | solution.py:24
  4.5 0.0 copy-start.1
  4.5 0.0 copy-start.2
  4.5 5.3 %all-to-all-start = ((bf16[8,96,2,512]{3,2,1,0:T(2,128)(2,1)}), bf16[8,96,2,512]{3,2,1,0:T(2,128)(2,1)S(1)}, u32[]{:S(2)}, u32[]{:S(2)}) async-start(bf16[8,96,2,512]{3,2,1,0:T(2,128)(2,1)} %reshape.104), calls=%async_computation | async-start | bytes 3145728 | tf_op jit(solution)/shard_map/all_to_all | solution.py:26
  9.8 0.0 copy-done.1
  9.8 0.1 copy.23
  9.9 0.1 reshape.102
  10.0 0.1 eq.26
  10.1 0.1 copy.27
  10.2 0.1 mul.115
  10.3 1.2 %reduce-window.6 = s32[64,4,128]{2,0,1:T(8,128)S(1)} reduce-window(s32[64,4,128]{2,0,1:T(8,128)S(1)} %fusion.2, s32[]{:T(128)} %constant.19.clone.1), window={size=1x1x128 pad=0_0x0_0x127_0}, to_apply=%region_0.0 | reduce-window | flops 4161536 | bytes 262148 | tf_op jit(solution)/shard_map/reduce-window
  11.5 0.2 slice_reduce_fusion
  11.8 0.2 convert_reduce_fusion
  12.0 0.1 reduce_sum.23
  12.1 0.1 copy.26
  12.1 40.4 %psum.7 = f32[64]{0:T(128)} all-reduce(f32[64]{0:T(128)S(1)} %convert_element_type.92), channel_id=1, replica_groups=mesh['dp'=4,'expert'=8] {'expert'}, use_global_device_ids=true, to_apply=%region_4.5 | all-reduce | flops 64 | bytes 512 | tf_op jit(solution)/shard_map/psum | solution.py:25
  52.6 0.0 copy-done.2
  52.6 0.0 all-to-all-done
  52.6 3.6 %gather_fusion = bf16[512,2,512]{2,1,0:T(2,128)(2,1)S(1)} fusion(bf16[768,2,512]{2,1,0:T(2,128)(2,1)S(1)} %bitcast.63, s32[1024]{0:T(1024)S(1)} %pad_clamp_fusion), kind=kCustom, calls=%fused_computation | custom fusion | bytes 2099200 | tf_op jit(solution)/shard_map/jit(_take)/gather | solution.py:29
  56.2 1.2 %copy_select_fusion = bf16[64,8,2,512]{3,0,2,1:T(8,128)(2,1)S(1)} fusion(bf16[64,8,2,512]{3,2,1,0:T(2,128)(2,1)S(1)} %bitcast.64, pred[64,8]{0,1:T(8,128)(4,1)S(1)} %compare_and_fusion), kind=kLoop, calls=%fused_computation.1 | loop fusion | flops 524288 | bytes 2097664 | tf_op jit(solution)/shard_map/jit(_take)/select_n | solution.py:29
  57.4 0.2 slice_convert_fusion.7
  57.7 0.2 copy.37
  57.9 0.2 copy.36
  58.2 0.2 copy.35
  58.5 0.2 copy.34
  58.7 0.2 copy.33
  59.0 0.0 copy-start
  59.0 0.2 copy.32
  59.3 0.2 copy.31
  59.6 0.2 copy.30
  59.8 0.1 copy-done
  59.9 0.9 %add_convert_fusion = bf16[64,1024]{1,0:T(8,128)(2,1)} fusion(bf16[64,1024]{1,0:T(8,128)(2,1)S(1)} %copy-done, f32[64,1024]{1,0:T(8,128)S(1)} %bitcast.65, f32[64,1024]{1,0:T(8,128)S(1)} %bitcast.66, f32[64,1024]{1,0:T(8,128)S(1)} %bitcast.67, f32[64,1024]{1,0:T(8,128)S(1)} %bitcast.68, f32[64,1024]{1,0:T(8,128)S(1)} %bitcast.69, f32[64,1024]{1,0:T(8,128)S(1)} %bitcast.70, ...), kind=kLoop, calls=%fused_computation.2 | loop fusion | flops 1179648 | bytes 2361344 | tf_op jit(solution)/shard_map/convert_element_type | solution.py:37
  (17 shorter events, 0.5 us)
Async XLA Ops:
  4.5 5.3 %copy-start.1 = (s32[64,8]{0,1:T(8,128)S(1)}, s32[64,8]{0,1:T(8,128)}, u32[]{:S(2)}) copy-start(s32[64,8]{0,1:T(8,128)} %param.5) | copy-start | bytes 6148
  4.5 48.1 %copy-start.2 = (f32[64,8]{0,1:T(8,128)S(1)}, f32[64,8]{0,1:T(8,128)}, u32[]{:S(2)}) copy-start(f32[64,8]{0,1:T(8,128)} %param.6) | copy-start | bytes 6148
  4.5 48.1 %all-to-all-start = ((bf16[8,96,2,512]{3,2,1,0:T(2,128)(2,1)}), bf16[8,96,2,512]{3,2,1,0:T(2,128)(2,1)S(1)}, u32[]{:S(2)}, u32[]{:S(2)}) async-start(bf16[8,96,2,512]{3,2,1,0:T(2,128)(2,1)} %reshape.104), calls=%async_computation | async-start | bytes 3145728 | tf_op jit(solution)/shard_map/all_to_all | solution.py:26
  59.0 0.9 %copy-start = (bf16[64,1024]{1,0:T(8,128)(2,1)S(1)}, bf16[64,1024]{1,0:T(8,128)(2,1)}, u32[]{:S(2)}) copy-start(bf16[64,1024]{1,0:T(8,128)(2,1)} %param.4) | copy-start | bytes 393220
where the time goes:
time: 61.1 us; the launch traced here: 60.8 us
  blocking collectives  40.4 us (66%)
  local copies, waits for them, and re-layouts  10.4 us (17%)
  starting transfers between devices  5.34 us (9%)
  other arithmetic  3.79 us (6%)
  between operations  0.84 us (1%)
    psum x1, blocking collectives, per_device(): load_totals = lax.psum(own_counts, 'expert')  40.4 us
    all_to_all x1, starting transfers between devices, per_device(): lax.all_to_all(blocks, 'expert', split_axis=0, concat_axis=0, tiled=True)  5.34 us
    reshape x1, local copies, waits for them, and re-layouts, per_device(): blocks = expert_out.reshape(peers, per_peer, column_blocks, block_width)  3.87 us
    gather x1, local copies, waits for them, and re-layouts, per_device(): jnp.take(stacked, source_rows, axis=0)  3.56 us
    convert_element_type x8, local copies, waits for them, and re-layouts, per_device(): picked[:, choice_index].astype(jnp.float32)  1.64 us
    another operation x2, other arithmetic  1.24 us
    select_n x2, other arithmetic, per_device(): jnp.take(stacked, source_rows, axis=0)  1.24 us
  transfers between devices with their start and end apart: 1, of which 0 were waited for; matrix products, arithmetic and copies ran while one was open for 4% of the time, Pallas kernels for 0%

commit v1 on v0

v1 whole, which is shorter than its diff:
```python
import functools
import jax
import jax.numpy as jnp
from jax import lax
from jax.experimental import pallas as pl
from jax.experimental.pallas import tpu as pltpu
from jax.sharding import PartitionSpec as P

EXPERTS = 64
CORES = 2
VMEM_BUDGET = 24 * 1024 * 1024


def dot(a, b, dims=(((1,), (0,)), ((), ()))):
    return lax.dot_general(a, b, dims, preferred_element_type=jnp.float32)


def combine_kernel(
    chips, capacity,
    ids_ref, weights_ref, residual_ref, rows_hbm,
    mixed_ref, load_ref,
    raw, ids_all, weights_all, partial, arrived, own_sum, counts, counts_in,
    local_sem, raw_send, raw_recv, ids_send, ids_recv, w_send, w_recv,
    out_send, out_recv, load_sems,
):
    me = lax.axis_index("expert")
    chip, core = me // CORES, me % CORES
    other = 1 - core
    partner = {"expert": chip * CORES + other}
    tokens, width = residual_ref.shape
    fanout = ids_ref.shape[0]
    per_peer = rows_hbm.shape[1]
    held = CORES * per_peer
    local_experts = held // capacity

    def peer(step):
        return lax.rem(chip + step, chips)

    def device(step):
        return {"expert": peer(step) * CORES + core}

    barrier = pltpu.get_barrier_semaphore()
    pl.semaphore_signal(barrier, inc=1, device_id=partner)
    for step in range(1, chips):
        pl.semaphore_signal(barrier, inc=1, device_id=device(step))

    local = []
    for j in range(chips):
        copy = pltpu.make_async_copy(rows_hbm.at[j * CORES + core], raw.at[j, core], local_sem.at[j])
        copy.start()
        local.append(copy)
    pl.semaphore_wait(barrier, chips)

    routing = []
    for step in range(1, chips):
        a = pltpu.make_async_remote_copy(
            ids_ref, ids_all.at[step], ids_send.at[step], ids_recv.at[step], device_id=device(step))
        b = pltpu.make_async_remote_copy(
            weights_ref, weights_all.at[step], w_send.at[step], w_recv.at[step], device_id=device(step))
        a.start()
        b.start()
        routing.append((a, b))
    rows = []
    for j in range(chips):
        copy = pltpu.make_async_remote_copy(
            rows_hbm.at[j * CORES + other], raw.at[j, core], raw_send.at[j], raw_recv.at[j],
            device_id=partner)
        copy.start()
        rows.append(copy)

    before = (lax.broadcasted_iota(jnp.int32, (tokens, tokens), 0)
              < lax.broadcasted_iota(jnp.int32, (tokens, tokens), 1)).astype(jnp.float32).astype(jnp.bfloat16)
    place = lax.broadcasted_iota(jnp.int32, (held, local_experts), 0)
    which = lax.broadcasted_iota(jnp.int32, (held, local_experts), 1)
    low = which * capacity
    spread = ((place >= low) & (place < low + capacity)).astype(jnp.float32).astype(jnp.bfloat16)
    wanted = (lax.broadcasted_iota(jnp.int32, (held, tokens), 0) % capacity).astype(jnp.float32)
    expert = lax.broadcasted_iota(jnp.int32, (local_experts, tokens), 0) + chip * local_experts

    def select(ids, weights):
        chosen = jnp.zeros((local_experts, tokens), jnp.float32)
        weight = jnp.zeros((local_experts, tokens), jnp.float32)
        for k in range(fanout):
            hit = ids[k:k + 1, :] == expert
            chosen = jnp.where(hit, 1.0, chosen)
            weight = jnp.where(hit, weights[k:k + 1, :], weight)
        slot = dot(chosen.astype(jnp.bfloat16), before)
        slot = jnp.where(chosen > 0, slot, -1.0)
        keep = dot(spread, slot.astype(jnp.bfloat16)) == wanted
        pieces = []
        rest = weight
        for _ in range(3):
            piece = rest.astype(jnp.bfloat16)
            rest = rest - piece.astype(jnp.float32)
            pieces.append(jnp.where(keep, dot(spread, piece), 0.0))
        return pieces

    def combine(pieces, block):
        total = None
        for piece in pieces:
            part = dot(jnp.transpose(piece).astype(jnp.bfloat16), block)
            total = part if total is None else total + part
        return total

    sends = []
    order = [chips // 2] + [s for s in range(1, chips) if s != chips // 2]
    for j in range(chips):
        local[j].wait()
        rows[j].wait()
    for step in order:
        routing[step - 1][0].wait()
        routing[step - 1][1].wait()
        j = lax.rem(chip + chips - step, chips)
        pieces = select(ids_all[step], weights_all[step])
        partial[step] = combine(pieces, raw[j].reshape(held, width))
        copy = pltpu.make_async_remote_copy(
            partial.at[step], arrived.at[step], out_send.at[step], out_recv.at[step],
            device_id=device(chips - step))
        copy.start()
        sends.append(copy)

    own_sum[...] = combine(select(ids_ref[...], weights_ref[...]), raw[chip].reshape(held, width))

    every = lax.broadcasted_iota(jnp.int32, (EXPERTS, tokens), 0)
    seen = jnp.zeros((EXPERTS, tokens), jnp.float32)
    for step in range(chips):
        ids = ids_ref[...] if step == 0 else ids_all[step]
        for k in range(fanout):
            seen = seen + jnp.where(ids[k:k + 1, :] == every, 1.0, 0.0)
    ones = jnp.ones((8, tokens), jnp.float32).astype(jnp.bfloat16)
    counts[...] = dot(ones, seen.astype(jnp.bfloat16), (((1,), (1,)), ((), ())))
    tally = pltpu.make_async_remote_copy(
        counts, counts_in, load_sems.at[0], load_sems.at[1], device_id=partner)
    tally.start()

    own_sum[...] = own_sum[...] + residual_ref[...].astype(jnp.float32)
    tally.wait()
    load_ref[...] = (counts[...] + counts_in[...])[0:1, :]
    for n, step in enumerate(order):
        sends[n].wait()
        own_sum[...] = own_sum[...] + arrived[step]
    mixed_ref[...] = own_sum[...].astype(jnp.bfloat16)


def fused(chips, residual, expert_ids, route_weights, expert_out):
    peers = chips * CORES
    tokens, width = residual.shape
    fanout = expert_ids.shape[1]
    per_peer = expert_out.shape[0] // peers
    capacity = expert_out.shape[0] // EXPERTS
    vmem = pl.BlockSpec(memory_space=pltpu.VMEM)
    dma = pltpu.SemaphoreType.DMA
    mixed, load = pl.pallas_call(
        functools.partial(combine_kernel, chips, capacity),
        out_shape=(
            jax.ShapeDtypeStruct((tokens, width), jnp.bfloat16),
            jax.ShapeDtypeStruct((1, EXPERTS), jnp.float32),
        ),
        in_specs=[vmem, vmem, vmem, pl.BlockSpec(memory_space=pl.ANY)],
        out_specs=(vmem, vmem),
        scratch_shapes=[
            pltpu.VMEM((chips, CORES, per_peer, width), jnp.bfloat16),
            pltpu.VMEM((chips, fanout, tokens), jnp.int32),
            pltpu.VMEM((chips, fanout, tokens), jnp.float32),
            pltpu.VMEM((chips, tokens, width), jnp.float32),
            pltpu.VMEM((chips, tokens, width), jnp.float32),
            pltpu.VMEM((tokens, width), jnp.float32),
            pltpu.VMEM((8, EXPERTS), jnp.float32),
            pltpu.VMEM((8, EXPERTS), jnp.float32),
        ] + [dma((chips,))] * 9 + [dma((2,))],
        compiler_params=pltpu.CompilerParams(collective_id=0, has_side_effects=True),
    )(expert_ids.T, route_weights.T, residual, expert_out.reshape(peers, per_peer, width))
    return mixed, load.reshape(EXPERTS)


def general(residual, expert_ids, route_weights, expert_out):
    peers = lax.axis_size("expert")
    per_peer = expert_out.shape[0] // peers
    width = residual.shape[1]
    tokens_here = expert_ids.shape[0]
    fanout = expert_ids.shape[1]
    capacity = expert_out.shape[0] // EXPERTS
    routes = expert_ids.reshape(-1)
    onehot = (routes[:, None] == jnp.arange(EXPERTS, dtype=jnp.int32)[None, :]).astype(jnp.int32)
    earlier = jnp.cumsum(onehot, axis=0, dtype=jnp.int32) - onehot
    slots = jnp.sum(earlier * onehot, axis=1, dtype=jnp.int32)
    source_rows = routes * capacity + slots
    load_totals = lax.psum(jnp.sum(onehot, axis=0).astype(jnp.float32), "expert")
    blocks = expert_out.reshape(peers, per_peer, width)
    arrived = lax.all_to_all(blocks, "expert", split_axis=0, concat_axis=0, tiled=True)
    picked = jnp.take(arrived.reshape(peers * per_peer, width), source_rows, axis=0)
    picked = picked.reshape(tokens_here, fanout, width)
    total = residual.astype(jnp.float32)
    for k in range(fanout):
        total = total + route_weights[:, k, None] * picked[:, k].astype(jnp.float32)
    return total.astype(jnp.bfloat16), load_totals


def solution(mesh):
    peers = mesh.shape["expert"]

    def per_device(residual, expert_ids, route_weights, expert_out):
        tokens, width = residual.shape
        slots = expert_out.shape[0]
        capacity, per_peer = slots // EXPERTS, slots // peers
        chips = peers // CORES
        needed = slots * width * 2 + (2 * chips + 4) * tokens * width * 4
        fits = (
            peers % CORES == 0 and chips > 1 and slots % EXPERTS == 0
            and per_peer % capacity == 0 and per_peer % 16 == 0 and needed <= VMEM_BUDGET
        )
        if fits:
            return fused(chips, residual, expert_ids, route_weights, expert_out)
        return general(residual, expert_ids, route_weights, expert_out)

    split = P(("dp", "expert"), None)
    return jax.shard_map(
        per_device,
        mesh=mesh,
        in_specs=(split,) * 4,
        out_specs=(split, P("dp")),
        check_vma=False,
    )
```

time: 61.1 us -> 35.7 us (0.58)
  the two profiles are of different devices: /device:TPU:16 before, /device:TPU:9 now
where the time goes in v1:
time: 35.7 us; the launch traced here: 35.5 us
  Pallas kernels  32.1 us (90%)
  local copies, waits for them, and re-layouts  2.74 us (8%)
  between operations  0.64 us (2%)
    pallas_call x1, Pallas kernels, fused(): pl.pallas_call(functools.partial(combine_kernel, chips, capacity), out_sh...  32.1 us
    unnamed x2, local copies, waits for them, and re-layouts  2.74 us

profile of v1, /device:TPU:9, one launch (start us, length us, event | category | flops | bytes accessed | tf_op | source)
XLA Modules:
  0.0 35.5 jit_solution(11506347367109394393)
XLA Ops:
  0.6 32.1 %shard_map.59 = (bf16[64,1024]{1,0:T(8,128)(2,1)}, f32[1,64]{1,0:T(1,128)}) custom-call(s32[8,64]{1,0:T(8,128)} %bitcast.5, f32[8,64]{1,0:T(8,128)} %bitcast.6, bf16[64,1024]{1,0:T(8,128)(2,1)} %residual_ref.1, bf16[8,96,1024]{2,1,0:T(8,128)(2,1)} %bitcast.4), custom_call_target="tpu_custom_call" | custom-call | tf_op jit(solution)/shard_map/pallas_call | solution.py:153
  32.7 1.6 %copy.8 = bf16[64,1024]{1,0:T(8,128)(2,1)} copy(bf16[64,1024]{1,0:T(8,128)(2,1)} %get-tuple-element.8) | data formatting | bytes 262144
  34.3 1.2 %copy.9 = f32[64]{0:T(128)} copy(f32[64]{0:T(128)} %bitcast.7) | data formatting | bytes 512

commit v2 on v1

--- a/solution.py
+++ b/solution.py
@@ -15,13 +15,28 @@
     return lax.dot_general(a, b, dims, preferred_element_type=jnp.float32)
 
 
+LEVELS = 32767.0
+
+
+def encode(x):
+    top = jnp.maximum(jnp.max(jnp.abs(x), axis=1, keepdims=True), 1e-30)
+    code = jnp.round(x * (LEVELS / top)).astype(jnp.int32).astype(jnp.int16)
+    scale = jnp.transpose(jnp.broadcast_to(top * (1.0 / LEVELS), (x.shape[0], 128)))[0:8, :]
+    return code, scale
+
+
+def decode(code, scale):
+    column = jnp.transpose(jnp.broadcast_to(scale[0:1, :], (128, scale.shape[1])))[:, 0:1]
+    return code.astype(jnp.int32).astype(jnp.float32) * column
+
+
 def combine_kernel(
     chips, capacity,
     ids_ref, weights_ref, residual_ref, rows_hbm,
     mixed_ref, load_ref,
-    raw, ids_all, weights_all, partial, arrived, own_sum, counts, counts_in,
+    raw, ids_all, weights_all, partial, arrived, scale_out, scale_in, own_sum, counts, counts_in,
     local_sem, raw_send, raw_recv, ids_send, ids_recv, w_send, w_recv,
-    out_send, out_recv, load_sems,
+    out_send, out_recv, scale_send, scale_recv, load_sems,
 ):
     me = lax.axis_index("expert")
     chip, core = me // CORES, me % CORES
@@ -112,12 +127,18 @@
         routing[step - 1][1].wait()
         j = lax.rem(chip + chips - step, chips)
         pieces = select(ids_all[step], weights_all[step])
-        partial[step] = combine(pieces, raw[j].reshape(held, width))
+        code, scale = encode(combine(pieces, raw[j].reshape(held, width)))
+        partial[step] = code
+        scale_out[step] = scale
+        small = pltpu.make_async_remote_copy(
+            scale_out.at[step], scale_in.at[step], scale_send.at[step], scale_recv.at[step],
+            device_id=device(chips - step))
+        small.start()
         copy = pltpu.make_async_remote_copy(
             partial.at[step], arrived.at[step], out_send.at[step], out_recv.at[step],
             device_id=device(chips - step))
         copy.start()
-        sends.append(copy)
+        sends.append((small, copy))
 
     own_sum[...] = combine(select(ids_ref[...], weights_ref[...]), raw[chip].reshape(held, width))
 
@@ -137,8 +158,9 @@
     tally.wait()
     load_ref[...] = (counts[...] + counts_in[...])[0:1, :]
     for n, step in enumerate(order):
-        sends[n].wait()
-        own_sum[...] = own_sum[...] + arrived[step]
+        sends[n][0].wait()
+        sends[n][1].wait()
+        own_sum[...] = own_sum[...] + decode(arrived[step], scale_in[step])
     mixed_ref[...] = own_sum[...].astype(jnp.bfloat16)
 
 
@@ -162,12 +184,14 @@
             pltpu.VMEM((chips, CORES, per_peer, width), jnp.bfloat16),
             pltpu.VMEM((chips, fanout, tokens), jnp.int32),
             pltpu.VMEM((chips, fanout, tokens), jnp.float32),
-            pltpu.VMEM((chips, tokens, width), jnp.float32),
-            pltpu.VMEM((chips, tokens, width), jnp.float32),
+            pltpu.VMEM((chips, tokens, width), jnp.int16),
+            pltpu.VMEM((chips, tokens, width), jnp.int16),
+            pltpu.VMEM((chips, 8, tokens), jnp.float32),
+            pltpu.VMEM((chips, 8, tokens), jnp.float32),
             pltpu.VMEM((tokens, width), jnp.float32),
             pltpu.VMEM((8, EXPERTS), jnp.float32),
             pltpu.VMEM((8, EXPERTS), jnp.float32),
-        ] + [dma((chips,))] * 9 + [dma((2,))],
+        ] + [dma((chips,))] * 11 + [dma((2,))],
         compiler_params=pltpu.CompilerParams(collective_id=0, has_side_effects=True),
     )(expert_ids.T, route_weights.T, residual, expert_out.reshape(peers, per_peer, width))
     return mixed, load.reshape(EXPERTS)

time: 35.7 us -> 25.4 us (0.71)
  the two profiles are of different devices: /device:TPU:9 before, /device:TPU:0 now
where the time goes in v2:
time: 25.4 us; the launch traced here: 25.2 us
  Pallas kernels  21.8 us (86%)
  local copies, waits for them, and re-layouts  2.74 us (11%)
  between operations  0.64 us (3%)
    pallas_call x1, Pallas kernels, fused(): pl.pallas_call(functools.partial(combine_kernel, chips, capacity), out_sh...  21.8 us
    unnamed x2, local copies, waits for them, and re-layouts  2.74 us

profile of v2, /device:TPU:0, one launch (start us, length us, event | category | flops | bytes accessed | tf_op | source)
XLA Modules:
  0.0 25.2 jit_solution(8518783443787982078)
XLA Ops:
  0.6 21.8 %shard_map.59 = (bf16[64,1024]{1,0:T(8,128)(2,1)}, f32[1,64]{1,0:T(1,128)}) custom-call(s32[8,64]{1,0:T(8,128)} %bitcast.5, f32[8,64]{1,0:T(8,128)} %bitcast.6, bf16[64,1024]{1,0:T(8,128)(2,1)} %residual_ref.1, bf16[8,96,1024]{2,1,0:T(8,128)(2,1)} %bitcast.4), custom_call_target="tpu_custom_call" | custom-call | tf_op jit(solution)/shard_map/pallas_call | solution.py:175
  22.5 1.6 %copy.8 = bf16[64,1024]{1,0:T(8,128)(2,1)} copy(bf16[64,1024]{1,0:T(8,128)(2,1)} %get-tuple-element.8) | data formatting | bytes 262144
  24.0 1.2 %copy.9 = f32[64]{0:T(128)} copy(f32[64]{0:T(128)} %bitcast.7) | data formatting | bytes 512

commit v3 on v2

--- a/solution.py
+++ b/solution.py
@@ -48,16 +48,39 @@
     held = CORES * per_peer
     local_experts = held // capacity
 
+    relayed = chips >= 4
+    last = chips - 1
+    at_end = (chip == 0) | (chip == last)
+    relays = (chip == 1) | (chip == last - 1)
+    far_end = last - chip
+    inner = jnp.where(chip == 0, 1, last - 1)
+
+    def by_chip(values):
+        out = jnp.int32(values[0])
+        for c in range(1, chips):
+            out = jnp.where(chip == c, values[c], out)
+        return out
+
+    def ordered(c):
+        others = [j for j in range(chips) if j != c]
+        middle = (chips - 1) / 2
+        if c in (0, chips - 1):
+            return sorted(others, key=lambda j: -abs(j - c))
+        return sorted(others, key=lambda j: (abs(j - c), abs(j - middle)))
+
+    tables = [ordered(c) for c in range(chips)]
+    targets = [by_chip([tables[c][n] for c in range(chips)]) for n in range(chips - 1)]
+
+    def device(j):
+        return {"expert": j * CORES + core}
+
     def peer(step):
         return lax.rem(chip + step, chips)
-
-    def device(step):
-        return {"expert": peer(step) * CORES + core}
 
     barrier = pltpu.get_barrier_semaphore()
     pl.semaphore_signal(barrier, inc=1, device_id=partner)
     for step in range(1, chips):
-        pl.semaphore_signal(barrier, inc=1, device_id=device(step))
+        pl.semaphore_signal(barrier, inc=1, device_id=device(peer(step)))
 
     local = []
     for j in range(chips):
@@ -66,15 +89,17 @@
         local.append(copy)
     pl.semaphore_wait(barrier, chips)
 
-    routing = []
+    def routing(slot, j):
+        return (
+            pltpu.make_async_remote_copy(
+                ids_ref, ids_all.at[slot], ids_send.at[j], ids_recv.at[slot], device_id=device(j)),
+            pltpu.make_async_remote_copy(
+                weights_ref, weights_all.at[slot], w_send.at[j], w_recv.at[slot], device_id=device(j)),
+        )
+
     for step in range(1, chips):
-        a = pltpu.make_async_remote_copy(
-            ids_ref, ids_all.at[step], ids_send.at[step], ids_recv.at[step], device_id=device(step))
-        b = pltpu.make_async_remote_copy(
-            weights_ref, weights_all.at[step], w_send.at[step], w_recv.at[step], device_id=device(step))
-        a.start()
-        b.start()
-        routing.append((a, b))
+        for copy in routing(chip, peer(step)):
+            copy.start()
     rows = []
     for j in range(chips):
         copy = pltpu.make_async_remote_copy(
@@ -117,35 +142,50 @@
             total = part if total is None else total + part
         return total
 
-    sends = []
-    order = [chips // 2] + [s for s in range(1, chips) if s != chips // 2]
+    def message(source, slot, to):
+        return (
+            pltpu.make_async_remote_copy(
+                scale_out.at[source], scale_in.at[slot], scale_send.at[source], scale_recv.at[slot],
+                device_id=device(to)),
+            pltpu.make_async_remote_copy(
+                partial.at[source], arrived.at[slot], out_send.at[source], out_recv.at[slot],
+                device_id=device(to)),
+        )
+
+    def take(slot):
+        for copy in message(0, slot, peer(1)):
+            copy.wait_recv()
+        return decode(arrived[slot], scale_in[slot])
+
     for j in range(chips):
         local[j].wait()
         rows[j].wait()
-    for step in order:
-        routing[step - 1][0].wait()
-        routing[step - 1][1].wait()
-        j = lax.rem(chip + chips - step, chips)
-        pieces = select(ids_all[step], weights_all[step])
-        code, scale = encode(combine(pieces, raw[j].reshape(held, width)))
-        partial[step] = code
-        scale_out[step] = scale
-        small = pltpu.make_async_remote_copy(
-            scale_out.at[step], scale_in.at[step], scale_send.at[step], scale_recv.at[step],
-            device_id=device(chips - step))
-        small.start()
-        copy = pltpu.make_async_remote_copy(
-            partial.at[step], arrived.at[step], out_send.at[step], out_recv.at[step],
-            device_id=device(chips - step))
-        copy.start()
-        sends.append((small, copy))
+    for n, j in enumerate(targets):
+        for copy in routing(j, j):
+            copy.wait_recv()
+        value = combine(select(ids_all[j], weights_all[j]), raw[j].reshape(held, width))
+        if relayed and n == chips - 2:
+            own_sum[...] = value
+
+            @pl.when(relays)
+            def _():
+                own_sum[...] = own_sum[...] + take(chips)
+
+            value = own_sum[...]
+        partial[n], scale_out[n] = encode(value)
+        to, slot = j, chip
+        if relayed and n == 0:
+            to, slot = jnp.where(at_end, inner, j), jnp.where(at_end, chips, chip)
+        for copy in message(n, slot, to):
+            copy.start()
 
     own_sum[...] = combine(select(ids_ref[...], weights_ref[...]), raw[chip].reshape(held, width))
+    own_sum[...] = own_sum[...] + residual_ref[...].astype(jnp.float32)
 
     every = lax.broadcasted_iota(jnp.int32, (EXPERTS, tokens), 0)
     seen = jnp.zeros((EXPERTS, tokens), jnp.float32)
     for step in range(chips):
-        ids = ids_ref[...] if step == 0 else ids_all[step]
+        ids = ids_ref[...] if step == 0 else ids_all[peer(step)]
         for k in range(fanout):
             seen = seen + jnp.where(ids[k:k + 1, :] == every, 1.0, 0.0)
     ones = jnp.ones((8, tokens), jnp.float32).astype(jnp.bfloat16)
@@ -153,15 +193,33 @@
     tally = pltpu.make_async_remote_copy(
         counts, counts_in, load_sems.at[0], load_sems.at[1], device_id=partner)
     tally.start()
-
-    own_sum[...] = own_sum[...] + residual_ref[...].astype(jnp.float32)
     tally.wait()
     load_ref[...] = (counts[...] + counts_in[...])[0:1, :]
-    for n, step in enumerate(order):
-        sends[n][0].wait()
-        sends[n][1].wait()
-        own_sum[...] = own_sum[...] + decode(arrived[step], scale_in[step])
+
+    for s in targets:
+        if relayed:
+            @pl.when(jnp.logical_not(at_end & (s == far_end)))
+            def _():
+                own_sum[...] = own_sum[...] + take(s)
+        else:
+            own_sum[...] = own_sum[...] + take(s)
     mixed_ref[...] = own_sum[...].astype(jnp.bfloat16)
+
+    for step in range(1, chips):
+        for copy in routing(chip, peer(step)):
+            copy.wait_send()
+    for n in range(chips - 1):
+        for copy in message(n, n, peer(1)):
+            copy.wait_send()
+
+
+def write_kernel(mixed_ref, load_ref, mixed_out, load_out, sems):
+    first = pltpu.make_async_copy(mixed_ref, mixed_out, sems.at[0])
+    second = pltpu.make_async_copy(load_ref, load_out, sems.at[1])
+    first.start()
+    second.start()
+    first.wait()
+    second.wait()
 
 
 def fused(chips, residual, expert_ids, route_weights, expert_out):
@@ -171,29 +229,39 @@
     per_peer = expert_out.shape[0] // peers
     capacity = expert_out.shape[0] // EXPERTS
     vmem = pl.BlockSpec(memory_space=pltpu.VMEM)
+    hbm = pl.BlockSpec(memory_space=pl.ANY)
     dma = pltpu.SemaphoreType.DMA
-    mixed, load = pl.pallas_call(
+    shapes = (
+        jax.ShapeDtypeStruct((tokens, width), jnp.bfloat16),
+        jax.ShapeDtypeStruct((1, EXPERTS), jnp.float32),
+    )
+    slots = chips + 1
+    results = pl.pallas_call(
         functools.partial(combine_kernel, chips, capacity),
-        out_shape=(
-            jax.ShapeDtypeStruct((tokens, width), jnp.bfloat16),
-            jax.ShapeDtypeStruct((1, EXPERTS), jnp.float32),
-        ),
-        in_specs=[vmem, vmem, vmem, pl.BlockSpec(memory_space=pl.ANY)],
+        out_shape=shapes,
+        in_specs=[vmem, vmem, vmem, hbm],
         out_specs=(vmem, vmem),
         scratch_shapes=[
             pltpu.VMEM((chips, CORES, per_peer, width), jnp.bfloat16),
             pltpu.VMEM((chips, fanout, tokens), jnp.int32),
             pltpu.VMEM((chips, fanout, tokens), jnp.float32),
             pltpu.VMEM((chips, tokens, width), jnp.int16),
-            pltpu.VMEM((chips, tokens, width), jnp.int16),
+            pltpu.VMEM((slots, tokens, width), jnp.int16),
             pltpu.VMEM((chips, 8, tokens), jnp.float32),
-            pltpu.VMEM((chips, 8, tokens), jnp.float32),
+            pltpu.VMEM((slots, 8, tokens), jnp.float32),
             pltpu.VMEM((tokens, width), jnp.float32),
             pltpu.VMEM((8, EXPERTS), jnp.float32),
             pltpu.VMEM((8, EXPERTS), jnp.float32),
-        ] + [dma((chips,))] * 11 + [dma((2,))],
+        ] + [dma((slots,))] * 11 + [dma((2,))],
         compiler_params=pltpu.CompilerParams(collective_id=0, has_side_effects=True),
     )(expert_ids.T, route_weights.T, residual, expert_out.reshape(peers, per_peer, width))
+    mixed, load = pl.pallas_call(
+        write_kernel,
+        out_shape=shapes,
+        in_specs=[vmem, vmem],
+        out_specs=(hbm, hbm),
+        scratch_shapes=[dma((2,))],
+    )(*results)
     return mixed, load.reshape(EXPERTS)
 
 

time: 25.4 us -> 24.7 us (0.972)
  local copies, waits for them, and re-layouts: 2.74 us -> 0 us
  Pallas kernels: 21.8 us -> 23.9 us
    unnamed x2 -> x0, local copies, waits for them, and re-layouts: 2.74 us -> none
    pallas_call x0 -> x1, Pallas kernels: none -> 1.58 us  [fused(): pl.pallas_call(write_kernel, out_shape=shapes, in_specs=[vmem, vmem], out...]
    pallas_call x1, Pallas kernels: 21.8 us -> 22.3 us  [fused(): pl.pallas_call(functools.partial(combine_kernel, chips, capacity), out_sh...]
where the time goes in v3:
time: 24.7 us; the launch traced here: 24.5 us
  Pallas kernels  23.9 us (97%)
  between operations  0.64 us (3%)
    pallas_call x1, Pallas kernels, fused(): pl.pallas_call(functools.partial(combine_kernel, chips, capacity), out_sh...  22.3 us
    pallas_call x1, Pallas kernels, fused(): pl.pallas_call(write_kernel, out_shape=shapes, in_specs=[vmem, vmem], out...  1.58 us

profile of v3, /device:TPU:0, one launch (start us, length us, event | category | flops | bytes accessed | tf_op | source)
XLA Modules:
  0.0 24.5 jit_solution(14817598592884976348)
XLA Ops:
  0.6 22.3 %shard_map.59 = (bf16[64,1024]{1,0:T(8,128)(2,1)}, f32[1,64]{1,0:T(1,128)}) custom-call(s32[8,64]{1,0:T(8,128)} %bitcast.5, f32[8,64]{1,0:T(8,128)} %bitcast.6, bf16[64,1024]{1,0:T(8,128)(2,1)} %residual_ref.1, bf16[8,96,1024]{2,1,0:T(8,128)(2,1)} %bitcast.4), custom_call_target="tpu_custom_call" | custom-call | tf_op jit(solution)/shard_map/pallas_call | solution.py:239
  22.9 1.6 %shard_map.60 = (bf16[64,1024]{1,0:T(8,128)(2,1)}, f32[1,64]{1,0:T(1,128)}) custom-call(bf16[64,1024]{1,0:T(8,128)(2,1)} %get-tuple-element.6.mixed_ref, f32[1,64]{1,0:T(1,128)} %get-tuple-element.7.load_ref), custom_call_target="tpu_custom_call" | custom-call | tf_op jit(solution)/shard_map/pallas_call | solution.py:258

commit v4 on v3

--- a/solution.py
+++ b/solution.py
@@ -32,11 +32,11 @@
 
 def combine_kernel(
     chips, capacity,
-    ids_ref, weights_ref, residual_ref, rows_hbm,
+    ids_hbm, weights_hbm, residual_hbm, rows_hbm,
     mixed_ref, load_ref,
-    raw, ids_all, weights_all, partial, arrived, scale_out, scale_in, own_sum, counts, counts_in,
+    ids_ref, weights_ref, residual_ref, raw, ids_all, weights_all, partial, arrived, scale_out, scale_in, own_sum, counts, counts_in,
     local_sem, raw_send, raw_recv, ids_send, ids_recv, w_send, w_recv,
-    out_send, out_recv, scale_send, scale_recv, load_sems,
+    out_send, out_recv, scale_send, scale_recv, load_sems, in_sems,
 ):
     me = lax.axis_index("expert")
     chip, core = me // CORES, me % CORES
@@ -82,11 +82,19 @@
     for step in range(1, chips):
         pl.semaphore_signal(barrier, inc=1, device_id=device(peer(step)))
 
+    fetched = []
+    for n, (source, target) in enumerate(
+            ((ids_hbm, ids_ref), (weights_hbm, weights_ref), (residual_hbm, residual_ref))):
+        copy = pltpu.make_async_copy(source, target, in_sems.at[n])
+        copy.start()
+        fetched.append(copy)
     local = []
     for j in range(chips):
         copy = pltpu.make_async_copy(rows_hbm.at[j * CORES + core], raw.at[j, core], local_sem.at[j])
         copy.start()
         local.append(copy)
+    fetched[0].wait()
+    fetched[1].wait()
     pl.semaphore_wait(barrier, chips)
 
     def routing(slot, j):
@@ -180,6 +188,7 @@
             copy.start()
 
     own_sum[...] = combine(select(ids_ref[...], weights_ref[...]), raw[chip].reshape(held, width))
+    fetched[2].wait()
     own_sum[...] = own_sum[...] + residual_ref[...].astype(jnp.float32)
 
     every = lax.broadcasted_iota(jnp.int32, (EXPERTS, tokens), 0)
@@ -238,10 +247,13 @@
     slots = chips + 1
     results = pl.pallas_call(
         functools.partial(combine_kernel, chips, capacity),
-        out_shape=shapes,
-        in_specs=[vmem, vmem, vmem, hbm],
+        out_shape=tuple(pltpu.VMEM(x.shape, x.dtype) for x in shapes),
+        in_specs=[hbm, hbm, hbm, hbm],
         out_specs=(vmem, vmem),
         scratch_shapes=[
+            pltpu.VMEM((fanout, tokens), jnp.int32),
+            pltpu.VMEM((fanout, tokens), jnp.float32),
+            pltpu.VMEM((tokens, width), jnp.bfloat16),
             pltpu.VMEM((chips, CORES, per_peer, width), jnp.bfloat16),
             pltpu.VMEM((chips, fanout, tokens), jnp.int32),
             pltpu.VMEM((chips, fanout, tokens), jnp.float32),
@@ -252,7 +264,7 @@
             pltpu.VMEM((tokens, width), jnp.float32),
             pltpu.VMEM((8, EXPERTS), jnp.float32),
             pltpu.VMEM((8, EXPERTS), jnp.float32),
-        ] + [dma((slots,))] * 11 + [dma((2,))],
+        ] + [dma((slots,))] * 11 + [dma((2,)), dma((3,))],
         compiler_params=pltpu.CompilerParams(collective_id=0, has_side_effects=True),
     )(expert_ids.T, route_weights.T, residual, expert_out.reshape(peers, per_peer, width))
     mixed, load = pl.pallas_call(
@@ -261,7 +273,7 @@
         in_specs=[vmem, vmem],
         out_specs=(hbm, hbm),
         scratch_shapes=[dma((2,))],
-    )(*results)
+    )(*[pltpu.with_memory_space_constraint(x, pltpu.VMEM) for x in results])
     return mixed, load.reshape(EXPERTS)
 
 

time: 24.7 us -> 22.2 us (0.90)
  Pallas kernels: 23.9 us -> 21.5 us
    pallas_call x1, Pallas kernels: 22.3 us -> 20.8 us  [fused(): pl.pallas_call(functools.partial(combine_kernel, chips, capacity), out_sh...]
    pallas_call x1, Pallas kernels: 1.58 us -> 0.68 us  [fused(): pl.pallas_call(write_kernel, out_shape=shapes, in_specs=[vmem, vmem], out...]
where the time goes in v4:
time: 22.2 us; the launch traced here: 22.1 us
  Pallas kernels  21.5 us (97%)
  between operations  0.64 us (3%)
    pallas_call x1, Pallas kernels, fused(): pl.pallas_call(functools.partial(combine_kernel, chips, capacity), out_sh...  20.8 us
    pallas_call x1, Pallas kernels, fused(): pl.pallas_call(write_kernel, out_shape=shapes, in_specs=[vmem, vmem], out...  0.68 us

profile of v4, /device:TPU:0, one launch (start us, length us, event | category | flops | bytes accessed | tf_op | source)
XLA Modules:
  0.0 22.1 jit_solution(15788599049720642312)
XLA Ops:
  0.6 20.8 %shard_map.59 = (bf16[64,1024]{1,0:T(8,128)(2,1)S(1)}, f32[1,64]{1,0:T(1,128)S(1)}) custom-call(s32[8,64]{1,0:T(8,128)} %bitcast.5, f32[8,64]{1,0:T(8,128)} %bitcast.6, bf16[64,1024]{1,0:T(8,128)(2,1)} %residual_hbm.1, bf16[8,96,1024]{2,1,0:T(8,128)(2,1)} %bitcast.4), custom_call_target="tpu_custom_call" | custom-call | tf_op jit(solution)/shard_map/pallas_call | solution.py:248
  21.4 0.7 %shard_map.60 = (bf16[64,1024]{1,0:T(8,128)(2,1)}, f32[1,64]{1,0:T(1,128)}) custom-call(bf16[64,1024]{1,0:T(8,128)(2,1)S(1)} %get-tuple-element.6.mixed_ref, f32[1,64]{1,0:T(1,128)S(1)} %get-tuple-element.7.load_ref), custom_call_target="tpu_custom_call" | custom-call | tf_op jit(solution)/shard_map/pallas_call | solution.py:270

commit v5 on v4

--- a/solution.py
+++ b/solution.py
@@ -16,6 +16,8 @@
 
 
 LEVELS = 32767.0
+PARTS = 2
+RELAY_TURN = 0
 
 
 def encode(x):
@@ -34,9 +36,9 @@
     chips, capacity,
     ids_hbm, weights_hbm, residual_hbm, rows_hbm,
     mixed_ref, load_ref,
-    ids_ref, weights_ref, residual_ref, raw, ids_all, weights_all, partial, arrived, scale_out, scale_in, own_sum, counts, counts_in,
+    ids_ref, weights_ref, residual_ref, staged, raw, ids_all, weights_all, partial, arrived, scale_out, scale_in, own_sum, counts, counts_in,
     local_sem, raw_send, raw_recv, ids_send, ids_recv, w_send, w_recv,
-    out_send, out_recv, scale_send, scale_recv, load_sems, in_sems,
+    out_send, out_recv, scale_send, scale_recv, stage_sems, load_sems, in_sems,
 ):
     me = lax.axis_index("expert")
     chip, core = me // CORES, me % CORES
@@ -71,6 +73,8 @@
     tables = [ordered(c) for c in range(chips)]
     targets = [by_chip([tables[c][n] for c in range(chips)]) for n in range(chips - 1)]
 
+    needed = targets + [chip]
+
     def device(j):
         return {"expert": j * CORES + core}
 
@@ -88,11 +92,22 @@
         copy = pltpu.make_async_copy(source, target, in_sems.at[n])
         copy.start()
         fetched.append(copy)
-    local = []
-    for j in range(chips):
-        copy = pltpu.make_async_copy(rows_hbm.at[j * CORES + core], raw.at[j, core], local_sem.at[j])
-        copy.start()
-        local.append(copy)
+    def outbound(n):
+        j = needed[n]
+        return pltpu.make_async_copy(rows_hbm.at[j * CORES + other], staged.at[n], stage_sems.at[n])
+
+    def inbound(n):
+        j = needed[n]
+        return pltpu.make_async_copy(rows_hbm.at[j * CORES + core], raw.at[j, core], local_sem.at[n])
+
+    def handed(n, slot):
+        return pltpu.make_async_remote_copy(
+            staged.at[n], raw.at[needed[n], slot], raw_send.at[n], raw_recv.at[n], device_id=partner)
+
+    for n in range(chips):
+        outbound(n).start()
+    for n in range(chips):
+        inbound(n).start()
     fetched[0].wait()
     fetched[1].wait()
     pl.semaphore_wait(barrier, chips)
@@ -108,13 +123,9 @@
     for step in range(1, chips):
         for copy in routing(chip, peer(step)):
             copy.start()
-    rows = []
-    for j in range(chips):
-        copy = pltpu.make_async_remote_copy(
-            rows_hbm.at[j * CORES + other], raw.at[j, core], raw_send.at[j], raw_recv.at[j],
-            device_id=partner)
-        copy.start()
-        rows.append(copy)
+    for n in range(chips):
+        outbound(n).wait()
+        handed(n, core).start()
 
     before = (lax.broadcasted_iota(jnp.int32, (tokens, tokens), 0)
               < lax.broadcasted_iota(jnp.int32, (tokens, tokens), 1)).astype(jnp.float32).astype(jnp.bfloat16)
@@ -144,49 +155,56 @@
         return pieces
 
     def combine(pieces, block):
-        total = None
-        for piece in pieces:
-            part = dot(jnp.transpose(piece).astype(jnp.bfloat16), block)
-            total = part if total is None else total + part
-        return total
-
-    def message(source, slot, to):
+        stacked = jnp.concatenate([jnp.transpose(piece) for piece in pieces], axis=0)
+        parts = dot(stacked.astype(jnp.bfloat16), block)
+        return parts[:tokens] + parts[tokens:2 * tokens] + parts[2 * tokens:]
+
+    size = tokens // PARTS
+
+    def message(source, slot, part, to):
         return (
             pltpu.make_async_remote_copy(
-                scale_out.at[source], scale_in.at[slot], scale_send.at[source], scale_recv.at[slot],
-                device_id=device(to)),
+                scale_out.at[source, part], scale_in.at[slot, part],
+                scale_send.at[source, part], scale_recv.at[slot, part], device_id=device(to)),
             pltpu.make_async_remote_copy(
-                partial.at[source], arrived.at[slot], out_send.at[source], out_recv.at[slot],
-                device_id=device(to)),
+                partial.at[source, part], arrived.at[slot, part],
+                out_send.at[source, part], out_recv.at[slot, part], device_id=device(to)),
         )
 
-    def take(slot):
-        for copy in message(0, slot, peer(1)):
+    def take(slot, part):
+        for copy in message(0, slot, part, peer(1)):
             copy.wait_recv()
-        return decode(arrived[slot], scale_in[slot])
-
-    for j in range(chips):
-        local[j].wait()
-        rows[j].wait()
+        return decode(arrived[slot, part], scale_in[slot, part])
+
     for n, j in enumerate(targets):
         for copy in routing(j, j):
             copy.wait_recv()
-        value = combine(select(ids_all[j], weights_all[j]), raw[j].reshape(held, width))
-        if relayed and n == chips - 2:
+        pieces = select(ids_all[j], weights_all[j])
+        inbound(n).wait()
+        handed(n, other).wait_recv()
+        value = combine(pieces, raw[j].reshape(held, width))
+        to, slot = j, chip
+        if relayed and n == RELAY_TURN:
+            to, slot = jnp.where(at_end, inner, j), jnp.where(at_end, chips, chip)
+        adds = relayed and n == chips - 2
+        if adds:
             own_sum[...] = value
-
-            @pl.when(relays)
-            def _():
-                own_sum[...] = own_sum[...] + take(chips)
-
-            value = own_sum[...]
-        partial[n], scale_out[n] = encode(value)
-        to, slot = j, chip
-        if relayed and n == 0:
-            to, slot = jnp.where(at_end, inner, j), jnp.where(at_end, chips, chip)
-        for copy in message(n, slot, to):
-            copy.start()
-
+        for part in range(PARTS):
+            span = slice(part * size, (part + 1) * size)
+            if adds:
+                @pl.when(relays)
+                def _():
+                    own_sum[span, :] = own_sum[span, :] + take(chips, part)
+
+                piece = own_sum[span, :]
+            else:
+                piece = value[span, :]
+            partial[n, part], scale_out[n, part] = encode(piece)
+            for copy in message(n, slot, part, to):
+                copy.start()
+
+    inbound(chips - 1).wait()
+    handed(chips - 1, other).wait_recv()
     own_sum[...] = combine(select(ids_ref[...], weights_ref[...]), raw[chip].reshape(held, width))
     fetched[2].wait()
     own_sum[...] = own_sum[...] + residual_ref[...].astype(jnp.float32)
@@ -205,21 +223,29 @@
     tally.wait()
     load_ref[...] = (counts[...] + counts_in[...])[0:1, :]
 
+    def add(s, part):
+        span = slice(part * size, (part + 1) * size)
+        own_sum[span, :] = own_sum[span, :] + take(s, part)
+
     for s in targets:
-        if relayed:
-            @pl.when(jnp.logical_not(at_end & (s == far_end)))
-            def _():
-                own_sum[...] = own_sum[...] + take(s)
-        else:
-            own_sum[...] = own_sum[...] + take(s)
+        for part in range(PARTS):
+            if relayed:
+                @pl.when(jnp.logical_not(at_end & (s == far_end)))
+                def _():
+                    add(s, part)
+            else:
+                add(s, part)
     mixed_ref[...] = own_sum[...].astype(jnp.bfloat16)
 
     for step in range(1, chips):
         for copy in routing(chip, peer(step)):
             copy.wait_send()
+    for n in range(chips):
+        handed(n, core).wait_send()
     for n in range(chips - 1):
-        for copy in message(n, n, peer(1)):
-            copy.wait_send()
+        for part in range(PARTS):
+            for copy in message(n, n, part, peer(1)):
+                copy.wait_send()
 
 
 def write_kernel(mixed_ref, load_ref, mixed_out, load_out, sems):
@@ -254,17 +280,18 @@
             pltpu.VMEM((fanout, tokens), jnp.int32),
             pltpu.VMEM((fanout, tokens), jnp.float32),
             pltpu.VMEM((tokens, width), jnp.bfloat16),
+            pltpu.VMEM((chips, per_peer, width), jnp.bfloat16),
             pltpu.VMEM((chips, CORES, per_peer, width), jnp.bfloat16),
             pltpu.VMEM((chips, fanout, tokens), jnp.int32),
             pltpu.VMEM((chips, fanout, tokens), jnp.float32),
-            pltpu.VMEM((chips, tokens, width), jnp.int16),
-            pltpu.VMEM((slots, tokens, width), jnp.int16),
-            pltpu.VMEM((chips, 8, tokens), jnp.float32),
-            pltpu.VMEM((slots, 8, tokens), jnp.float32),
+            pltpu.VMEM((chips, PARTS, tokens // PARTS, width), jnp.int16),
+            pltpu.VMEM((slots, PARTS, tokens // PARTS, width), jnp.int16),
+            pltpu.VMEM((chips, PARTS, 8, tokens // PARTS), jnp.float32),
+            pltpu.VMEM((slots, PARTS, 8, tokens // PARTS), jnp.float32),
             pltpu.VMEM((tokens, width), jnp.float32),
             pltpu.VMEM((8, EXPERTS), jnp.float32),
             pltpu.VMEM((8, EXPERTS), jnp.float32),
-        ] + [dma((slots,))] * 11 + [dma((2,)), dma((3,))],
+        ] + [dma((slots,))] * 7 + [dma((slots, PARTS))] * 4 + [dma((chips,)), dma((2,)), dma((3,))],
         compiler_params=pltpu.CompilerParams(collective_id=0, has_side_effects=True),
     )(expert_ids.T, route_weights.T, residual, expert_out.reshape(peers, per_peer, width))
     mixed, load = pl.pallas_call(
@@ -308,10 +335,10 @@
         slots = expert_out.shape[0]
         capacity, per_peer = slots // EXPERTS, slots // peers
         chips = peers // CORES
-        needed = slots * width * 2 + (2 * chips + 4) * tokens * width * 4
+        needed = 2 * slots * width * 2 + (2 * chips + 4) * tokens * width * 4
         fits = (
             peers % CORES == 0 and chips > 1 and slots % EXPERTS == 0
-            and per_peer % capacity == 0 and per_peer % 16 == 0 and needed <= VMEM_BUDGET
+            and per_peer % capacity == 0 and per_peer % 16 == 0 and tokens % (16 * PARTS) == 0 and needed <= VMEM_BUDGET
         )
         if fits:
             return fused(chips, residual, expert_ids, route_weights, expert_out)

time: 22.2 us -> 22.2 us (level)
  no operation moved by 1% of the time
where the time goes in v5:
time: 22.2 us; the launch traced here: 22 us
  Pallas kernels  21.4 us (96%)
  between operations  0.64 us (3%)
    pallas_call x1, Pallas kernels, fused(): pl.pallas_call(functools.partial(combine_kernel, chips, capacity), out_sh...  20.7 us
    pallas_call x1, Pallas kernels, fused(): pl.pallas_call(write_kernel, out_shape=shapes, in_specs=[vmem, vmem], out...  0.68 us

profile of v5, /device:TPU:0, one launch (start us, length us, event | category | flops | bytes accessed | tf_op | source)
XLA Modules:
  0.0 22.0 jit_solution(10414611907598555904)
XLA Ops:
  0.6 20.7 %shard_map.59 = (bf16[64,1024]{1,0:T(8,128)(2,1)S(1)}, f32[1,64]{1,0:T(1,128)S(1)}) custom-call(s32[8,64]{1,0:T(8,128)} %bitcast.5, f32[8,64]{1,0:T(8,128)} %bitcast.6, bf16[64,1024]{1,0:T(8,128)(2,1)} %residual_hbm.1, bf16[8,96,1024]{2,1,0:T(8,128)(2,1)} %bitcast.4), custom_call_target="tpu_custom_call" | custom-call | tf_op jit(solution)/shard_map/pallas_call | solution.py:274
  21.4 0.7 %shard_map.60 = (bf16[64,1024]{1,0:T(8,128)(2,1)}, f32[1,64]{1,0:T(1,128)}) custom-call(bf16[64,1024]{1,0:T(8,128)(2,1)S(1)} %get-tuple-element.6.mixed_ref, f32[1,64]{1,0:T(1,128)S(1)} %get-tuple-element.7.load_ref), custom_call_target="tpu_custom_call" | custom-call | tf_op jit(solution)/shard_map/pallas_call | solution.py:297
